TPU v7x, 32 devices: a whole 2x2x4 slice. The times are simulated.
32 devices in a mesh: section: 2 (over y), tensor: 16 (over z, x, core).
Axes of the slice: x: 2, y: 2, z: 4, core: 2. Of those that a mesh axis runs over, the one named last changes fastest.
Arguments:
- embedded: bfloat16 [32, 6144], P(None, 'tensor'), may hold values from -6 to 6
- norm_gain: float32 [2, 6144], P('section'), may hold values from 0.25 to 1.75
- qkv_weight: bfloat16 [2, 6144, 3, 4096], P('section', None, None, 'tensor'), may hold values from -0.078125 to 0.078125
- out_weight: bfloat16 [2, 4096, 6144], P('section', 'tensor'), may hold values from -0.09375 to 0.09375
- cache_keys: bfloat16 [2, 32, 256, 4096], P('section', None, None, 'tensor'), may hold values from -6 to 6
- cache_values: bfloat16 [2, 32, 256, 4096], P('section', None, None, 'tensor'), may hold values from -6 to 6
- dwa_weights: float32 [3, 4], replicated, may hold values from 0.05 to 0.45
- dwa_sources: int32 [3, 4], replicated, may hold values from 0 to 2, as said below
- token_order: int32 [32], replicated, may hold values from 0 to 31, each once
- kv_lengths: int32 [32], replicated, may hold values from 1 to 256, as said below
Outputs:
- final_mix: bfloat16 [32, 6144], P('section', 'tensor')
Inputs may be any that keep to these rules, and one draw needn't show every extreme that they name: `dwa_sources`: each entry of row i lies in 0 to i, and the first entry of row i is i. `token_order`: a permutation of 0 to 31. `kv_lengths`: some token sees all 256 positions.
All inputs are finite; a program needn't handle non-finite values.
Results may differ from a plain program's by a relative error of at most 0.025.
Values may be sent and summed in bfloat16 or wider, within the bound.
A program may use at most 128 MiB of HBM per device.

v0:
```python
import jax
import jax.numpy as jnp
from jax import lax
from jax.sharding import PartitionSpec as P

HD = 128


def broadcast(value, axis, root):
    mine = lax.axis_index(axis) == root
    return lax.psum(jnp.where(mine, value, jnp.zeros_like(value)), axis)


def coefficients(dwa_weights, dwa_sources, count):
    levels = jnp.arange(count, dtype=jnp.int32)
    matches = (dwa_sources[:, :, None] == levels[None, None, :]).astype(jnp.float32)
    return jnp.sum(dwa_weights[:, :, None] * matches, axis=1)


def attend(normed, qkv_local, key_rows, value_rows, lengths):
    row_count = normed.shape[0]
    heads_here = qkv_local.shape[-1] // HD
    projected = jnp.dot(
        normed, qkv_local.reshape(normed.shape[1], -1), preferred_element_type=jnp.float32
    )
    projected = projected.reshape(row_count, 3, heads_here, HD)
    query_rows = (projected[:, 0] * HD ** (-0.5)).astype(jnp.bfloat16)
    key_new = projected[:, 1].astype(jnp.bfloat16)
    value_new = projected[:, 2].astype(jnp.bfloat16)
    cache_len = key_rows.shape[1]
    key_rows = key_rows.reshape(row_count, cache_len, heads_here, HD)
    value_rows = value_rows.reshape(row_count, cache_len, heads_here, HD)
    scores = jnp.einsum("bhd,bchd->bhc", query_rows, key_rows, preferred_element_type=jnp.float32)
    own_score = jnp.sum(query_rows.astype(jnp.float32) * key_new.astype(jnp.float32), axis=-1)
    visible = jnp.arange(cache_len, dtype=jnp.int32)[None, None, :] < lengths[:, None, None]
    weights = jnp.where(visible, jnp.exp(scores), 0.0)
    own_weight = jnp.exp(own_score)
    denominator = jnp.sum(weights, axis=-1) + own_weight
    attended = jnp.einsum(
        "bhc,bchd->bhd",
        weights.astype(jnp.bfloat16),
        value_rows,
        preferred_element_type=jnp.float32,
    )
    attended = attended + own_weight.astype(jnp.bfloat16).astype(jnp.float32)[
        :, :, None
    ] * value_new.astype(jnp.float32)
    return (
        (attended / denominator[:, :, None])
        .astype(jnp.bfloat16)
        .reshape(row_count, heads_here * HD)
    )


def layer_step(
    layer_input,
    norm_gain,
    qkv_weight,
    out_weight,
    cache_keys,
    cache_values,
    token_order,
    kv_lengths,
):
    gathered = lax.all_gather(layer_input, "tensor", axis=1, tiled=True)
    floats = gathered.astype(jnp.float32)
    inv_rms = lax.rsqrt(jnp.mean(floats * floats, axis=-1, keepdims=True) + 1e-05)
    normed = (floats * inv_rms * norm_gain[0][None, :]).astype(jnp.bfloat16)
    key_rows = jnp.take(cache_keys[0], token_order, axis=0)
    value_rows = jnp.take(cache_values[0], token_order, axis=0)
    attended = attend(normed, qkv_weight[0], key_rows, value_rows, kv_lengths)
    partial_value = jnp.dot(attended, out_weight[0], preferred_element_type=jnp.float32)
    summed = lax.psum_scatter(
        partial_value.astype(jnp.bfloat16), "tensor", scatter_dimension=1, tiled=True
    ).astype(jnp.float32)
    return (layer_input.astype(jnp.float32) + summed).astype(jnp.bfloat16)


def per_device(
    embedded,
    norm_gain,
    qkv_weight,
    out_weight,
    cache_keys,
    cache_values,
    dwa_weights,
    dwa_sources,
    token_order,
    kv_lengths,
):
    sections = lax.axis_size("section")
    section_index = lax.axis_index("section")
    batch_rows = embedded.shape[0]
    coef_table = coefficients(dwa_weights, dwa_sources, sections + 1)
    own_coef = lax.dynamic_index_in_dim(coef_table, section_index, 0, keepdims=False)
    final_coef = coef_table[sections]
    start_floats = embedded.astype(jnp.float32)

    def run_layer(layer_input):
        return layer_step(
            layer_input,
            norm_gain,
            qkv_weight,
            out_weight,
            cache_keys,
            cache_values,
            token_order,
            kv_lengths,
        )

    def whole_step(step_index, carry):
        running, final_sum = carry
        produced = run_layer(running.astype(jnp.bfloat16))
        received = broadcast(produced, "section", step_index).astype(jnp.float32)
        running = running + own_coef[step_index + 1] * received
        final_sum = final_sum + final_coef[step_index + 1] * received
        return (running, final_sum)

    running, final_sum = lax.fori_loop(
        0, sections, whole_step, (own_coef[0] * start_floats, final_coef[0] * start_floats)
    )
    out_rows = batch_rows // sections
    mine = lax.dynamic_slice_in_dim(final_sum, section_index * out_rows, out_rows, 0)
    return mine.astype(jnp.bfloat16)


def solution(mesh):
    placed = (
        P(None, "tensor"),
        P("section", None),
        P("section", None, None, "tensor"),
        P("section", "tensor", None),
        P("section", None, None, "tensor"),
        P("section", None, None, "tensor"),
        P(),
        P(),
        P(),
        P(),
    )
    return jax.shard_map(
        per_device, mesh=mesh, in_specs=placed, out_specs=P("section", "tensor"), check_vma=False
    )
```

profile of v0, /device:TPU:0, one launch (start us, length us, event | category | flops | bytes accessed | tf_op | source)
XLA Modules:
  0.0 272.0 jit_solution(9310334494664870146)
XLA Ops:
  7.8 2.0 convert_multiply_fusion.6
  10.5 5.1 %gather_fusion = bf16[32,256,256]{2,1,0:T(8,128)(2,1)} fusion(bf16[32,256,256]{2,1,0:T(8,128)(2,1)} %bitcast.128, s32[1024]{0:T(1024)S(1)} %pad_clamp_fusion), kind=kCustom, calls=%fused_computation.clone | custom fusion | bytes 8388736 | tf_op jit(solution)/shard_map/while/body/eval_jaxpr/jit(_take)/gather | solution.py:69
  15.6 5.0 %gather_fusion.1 = bf16[32,256,256]{2,1,0:T(8,128)(2,1)} fusion(bf16[32,256,256]{2,1,0:T(8,128)(2,1)} %bitcast.129, s32[1024]{0:T(1024)S(1)} %pad_clamp_fusion), kind=kCustom, calls=%fused_computation.1.clone | custom fusion | bytes 8388736 | tf_op jit(solution)/shard_map/while/body/eval_jaxpr/jit(_take)/gather | solution.py:70
  20.6 6.0 %broadcast_select_fusion = (bf16[32,256,256]{2,1,0:T(8,128)(2,1)}, bf16[32,256,256]{2,1,0:T(8,128)(2,1)}) fusion(bf16[32,256,256]{2,1,0:T(8,128)(2,1)} %gather_fusion.1, pred[32]{0:T(512)(128)(4,1)S(1)} %compare_and_fusion, bf16[32,256,256]{2,1,0:T(8,128)(2,1)} %gather_fusion), kind=kLoop, calls=%fused_computation.49 | loop fusion | flops 4194304 | bytes 16777248 | tf_op jit(solution)/shard_map/while/body/eval_jaxpr/jit(_take)/select_n | solution.py:70
  26.6 12.8 %copy.17 = bf16[1,6144,3,256]{1,3,2,0:T(8,128)(2,1)} copy(bf16[1,6144,3,256]{3,1,2,0:T(8,128)(2,1)} %param.16) | data formatting | bytes 18874368 | tf_op jit(solution)/shard_map/while | solution.py:119
  39.5 224.4 %while.17 = (s32[]{:T(128)}, f32[32,384]{1,0:T(8,128)}, f32[32,384]{1,0:T(8,128)}, f32[3]{0:T(128)S(1)}, s32[32]{0:T(128)S(1)}, /*index=5*/f32[1,6144]{1,0:T(1,1...) while((s32[]{:T(128)}, f32[32,384]{1,0:T(8,128)}, ...), condition=%wide.region_7.9_spmd, body=%wide.region_1.8_spmd.sunk | while | flops 412962912 | bytes 52300772 | solution.py:119
  40.3 24.1 %all_gather.11 = bf16[32,6144]{1,0:T(8,128)(2,1)S(1)} all-gather(bf16[32,384]{1,0:T(8,128)(2,1)S(1)} %convert_element_type.296), channel_id=1, replica_groups=mesh['section'=2,'tensor'=16] {'tensor'}, dimensions={1}, use_global_device_ids=true | all-gather | bytes 417792 | tf_op jit(solution)/shard_map/while/body/eval_jaxpr/all_gather | solution.py:65
  64.7 5.4 %fusion.67 = (bf16[32,3,2,128]{3,0,2,1:T(8,128)(2,1)S(1)}, f32[32,3,2,128]{3,0,2,1:T(8,128)S(1)}) fusion(bf16[3,2,128,6144]{3,2,1,0:T(8,128)(2,1)} %bitcast.126, bf16[32,6144]{1,0:T(8,128)(2,1)S(1)} %all_gather.11, f32[6144]{0:T(1024)} %bitcast.119, f32[32]{0:T(128)S(1)} %add_rsqrt_fusion.2), kind=kOutput, calls=%fused_computation.61.clone.1 | convolution fusion | flops 302800896 | bytes 10002560 | tf_op jit(solution)/shard_map/while/body/eval_jaxpr/dot_general | solution.py:23
  70.7 6.5 %copy.69 = bf16[32,256,256]{1,2,0:T(8,128)(2,1)} copy(bf16[32,256,256]{2,1,0:T(8,128)(2,1)} %get-tuple-element.496) | data formatting | bytes 8388608 | tf_op jit(solution)/shard_map/while/body/eval_jaxpr/reshape | solution.py:31
  77.2 3.0 %fusion.70 = f32[32,2,1,256]{3,2,1,0:T(1,128)S(1)} fusion(bf16[32,256,2,128]{1,3,2,0:T(8,128)(2,1)} %bitcast.125, bf16[32,2,128,1]{2,0,1,3:T(8,128)(2,1)S(1)} %fusion.69), kind=kOutput, calls=%fused_computation.35.clone.1 | convolution fusion | flops 4194304 | bytes 4276224 | tf_op jit(solution)/shard_map/while/body/eval_jaxpr/bhd,bchd->bhc/dot_general | solution.py:33
  81.3 1.4 convolution_convert_fusion.2
  82.7 1.5 copy.70
  85.5 55.7 %reduce-scatter.6.cloned.1.call-done = bf16[384,32]{1,0:T(8,128)(2,1)} async-done(((bf16[6144,32]{1,0:T(8,128)(2,1)}), bf16[384,32]{1,0:T(8,128)(2,1)}) %reduce-scatter.6.cloned.1.call-update) | async-done | bytes 24592 | tf_op jit(solution)/shard_map/while
  143.0 8.3 %psum.15 = bf16[32,384]{1,0:T(8,128)(2,1)S(1)} all-reduce(bf16[32,384]{1,0:T(8,128)(2,1)S(1)} %fusion.74), channel_id=1, replica_groups=mesh['section'=2,'tensor'=16] {'section'}, use_global_device_ids=true, to_apply=%region_6.7 | all-reduce | flops 12288 | bytes 49152 | tf_op jit(solution)/shard_map/while/body/eval_jaxpr/psum | solution.py:11
  151.2 2.8 %fusion.75 = (f32[32,384]{1,0:T(8,128)}, f32[32,384]{1,0:T(8,128)}) fusion(f32[32,384]{1,0:T(8,128)} %get-tuple-element.475, bf16[32,384]{1,0:T(8,128)(2,1)S(1)} %psum.15, f32[]{:T(128)} %bitcast.123, f32[32,384]{1,0:T(8,128)} %get-tuple-element.474, f32[]{:T(128)} %bitcast.124), kind=kLoop, calls=%fused_computation.24.clone.1 | loop fusion | flops 61440 | bytes 221192 | tf_op jit(solution)/shard_map/while/body/eval_jaxpr/add | solution.py:116
  154.8 20.4 %all_gather.11 = bf16[32,6144]{1,0:T(8,128)(2,1)S(1)} all-gather(bf16[32,384]{1,0:T(8,128)(2,1)S(1)} %convert_element_type.296), channel_id=1, replica_groups=mesh['section'=2,'tensor'=16] {'tensor'}, dimensions={1}, use_global_device_ids=true | all-gather | bytes 417792 | tf_op jit(solution)/shard_map/while/body/eval_jaxpr/all_gather | solution.py:65
  175.5 5.4 %fusion.67 = (bf16[32,3,2,128]{3,0,2,1:T(8,128)(2,1)S(1)}, f32[32,3,2,128]{3,0,2,1:T(8,128)S(1)}) fusion(bf16[3,2,128,6144]{3,2,1,0:T(8,128)(2,1)} %bitcast.126, bf16[32,6144]{1,0:T(8,128)(2,1)S(1)} %all_gather.11, f32[6144]{0:T(1024)} %bitcast.119, f32[32]{0:T(128)S(1)} %add_rsqrt_fusion.2), kind=kOutput, calls=%fused_computation.61.clone.1 | convolution fusion | flops 302800896 | bytes 10002560 | tf_op jit(solution)/shard_map/while/body/eval_jaxpr/dot_general | solution.py:23
  181.5 6.5 %copy.69 = bf16[32,256,256]{1,2,0:T(8,128)(2,1)} copy(bf16[32,256,256]{2,1,0:T(8,128)(2,1)} %get-tuple-element.496) | data formatting | bytes 8388608 | tf_op jit(solution)/shard_map/while/body/eval_jaxpr/reshape | solution.py:31
  188.0 3.0 %fusion.70 = f32[32,2,1,256]{3,2,1,0:T(1,128)S(1)} fusion(bf16[32,256,2,128]{1,3,2,0:T(8,128)(2,1)} %bitcast.125, bf16[32,2,128,1]{2,0,1,3:T(8,128)(2,1)S(1)} %fusion.69), kind=kOutput, calls=%fused_computation.35.clone.1 | convolution fusion | flops 4194304 | bytes 4276224 | tf_op jit(solution)/shard_map/while/body/eval_jaxpr/bhd,bchd->bhc/dot_general | solution.py:33
  192.0 1.4 convolution_convert_fusion.2
  193.5 1.5 copy.70
  196.3 54.7 %reduce-scatter.6.cloned.1.call-done = bf16[384,32]{1,0:T(8,128)(2,1)} async-done(((bf16[6144,32]{1,0:T(8,128)(2,1)}), bf16[384,32]{1,0:T(8,128)(2,1)}) %reduce-scatter.6.cloned.1.call-update) | async-done | bytes 24592 | tf_op jit(solution)/shard_map/while
  252.8 8.3 %psum.15 = bf16[32,384]{1,0:T(8,128)(2,1)S(1)} all-reduce(bf16[32,384]{1,0:T(8,128)(2,1)S(1)} %fusion.74), channel_id=1, replica_groups=mesh['section'=2,'tensor'=16] {'section'}, use_global_device_ids=true, to_apply=%region_6.7 | all-reduce | flops 12288 | bytes 49152 | tf_op jit(solution)/shard_map/while/body/eval_jaxpr/psum | solution.py:11
  261.1 2.8 %fusion.75 = (f32[32,384]{1,0:T(8,128)}, f32[32,384]{1,0:T(8,128)}) fusion(f32[32,384]{1,0:T(8,128)} %get-tuple-element.475, bf16[32,384]{1,0:T(8,128)(2,1)S(1)} %psum.15, f32[]{:T(128)} %bitcast.123, f32[32,384]{1,0:T(8,128)} %get-tuple-element.474, f32[]{:T(128)} %bitcast.124), kind=kLoop, calls=%fused_computation.24.clone.1 | loop fusion | flops 61440 | bytes 221192 | tf_op jit(solution)/shard_map/while/body/eval_jaxpr/add | solution.py:116
  (51 shorter events, 14.9 us)
Async XLA Ops:
  15.6 5.0 %copy-start.4 = (s32[32]{0:T(128)S(1)}, s32[32]{0:T(128)}, u32[]{:S(2)}) copy-start(s32[32]{0:T(128)} %param.22) | copy-start | bytes 388
  26.6 12.8 %copy-start = (bf16[1,256,6144]{2,1,0:T(8,128)(2,1)S(1)}, bf16[1,256,6144]{2,1,0:T(8,128)(2,1)}, u32[]{:S(2)}) copy-start(bf16[1,256,6144]{2,1,0:T(8,128)(2,1)} %param.17) | copy-start | bytes 9437188
  26.6 12.8 %copy-start.3 = (s32[32]{0:T(128)S(1)}, s32[32]{0:T(128)}, u32[]{:S(2)}) copy-start(s32[32]{0:T(128)} %param.23) | copy-start | bytes 388
  39.5 101.7 %reduce-scatter.6.cloned.1.call-start = ((), (), s32[]{:S(2)}) async-start(), calls=%async_computation.1 | async-start | bytes 1671168 | tf_op jit(solution)/shard_map/while
  70.1 0.6 copy-start.2
  77.2 3.4 %copy-start.1 = (bf16[32,256,256]{2,1,0:T(8,128)(2,1)S(1)}, bf16[32,256,256]{2,1,0:T(8,128)(2,1)}, u32[]{:S(2)}) copy-start(bf16[32,256,256]{2,1,0:T(8,128)(2,1)} %get-tuple-element.497) | copy-start | bytes 12582916 | tf_op jit(solution)/shard_map/while
  154.0 97.0 %reduce-scatter.6.cloned.1.call-start = ((), (), s32[]{:S(2)}) async-start(), calls=%async_computation.1 | async-start | bytes 1671168 | tf_op jit(solution)/shard_map/while
  180.9 0.6 copy-start.2
  188.0 3.4 %copy-start.1 = (bf16[32,256,256]{2,1,0:T(8,128)(2,1)S(1)}, bf16[32,256,256]{2,1,0:T(8,128)(2,1)}, u32[]{:S(2)}) copy-start(bf16[32,256,256]{2,1,0:T(8,128)(2,1)} %get-tuple-element.497) | copy-start | bytes 12582916 | tf_op jit(solution)/shard_map/while
Sparse Core Ops, SparseCore 0:
  84.3 56.7 reduce-scatter.5
  195.1 55.8 reduce-scatter.5
where the time goes:
time: 273 us; the launch traced here: 272 us
  waiting for transfers between devices  110 us (40%)
  blocking collectives  61.1 us (22%)
  local copies, waits for them, and re-layouts  46.8 us (17%)
  matrix products  20.8 us (8%)
  other arithmetic  19.3 us (7%)
  between operations  13.4 us (5%)
    while x4, waiting for transfers between devices  110 us
    all_gather x2, blocking collectives, layer_step(): gathered = lax.all_gather(layer_input, 'tensor', axis=1, tiled=True)  44.6 us
    psum x2, blocking collectives, broadcast(): return lax.psum(jnp.where(mine, value, jnp.zeros_like(value)), axis)  16.6 us
    reshape x2, local copies, waits for them, and re-layouts, attend(): key_rows = key_rows.reshape(row_count, cache_len, heads_here, HD)  13 us
    while x1, local copies, waits for them, and re-layouts, per_device(): lax.fori_loop(0, sections, whole_step, (own_coef[0] * start_floats, final...  12.8 us
    dot_general x2, matrix products, attend(): jnp.dot(normed, qkv_local.reshape(normed.shape[1], -1), preferred_element...  10.8 us
    while x12, local copies, waits for them, and re-layouts  6.55 us
    select_n x1, other arithmetic, layer_step(): value_rows = jnp.take(cache_values[0], token_order, axis=0)  5.97 us
  transfers between devices with their start and end apart: 2, of which 2 were waited for; matrix products, arithmetic and copies ran while one was open for 1% of the time, Pallas kernels for 0%

commit v1 on v0

v1 whole, which is shorter than its diff:
```python
import functools

import jax
import jax.numpy as jnp
from jax import lax
from jax.experimental import pallas as pl
from jax.experimental.pallas import tpu as pltpu
from jax.sharding import PartitionSpec as P

HD = 128
SUB = 8
MESH = pl.DeviceIdType.MESH
F32 = jnp.float32
BF16 = jnp.bfloat16


def kernel(
    sections,
    tensors,
    emb_ref,
    gain_ref,
    w_hbm,
    wo_hbm,
    k_hbm,
    v_hbm,
    dw_ref,
    ds_ref,
    order_ref,
    len_ref,
    out_ref,
    w_ref,
    wo_ref,
    k_ref,
    v_ref,
    g_ref,
    fin_ref,
    acc_ref,
    x_ref,
    q_ref,
    s_ref,
    p_ref,
    d_ref,
    o_ref,
    part_ref,
    pair_ref,
    ps_ref,
    rs_ref,
    outb_ref,
    mix_ref,
    loc_sem,
    g_recv,
    g_send,
    fwd_send,
    pair_send,
    pair_recv,
    rs_send,
    rs_recv,
    bc_send,
    fin_send,
    fin_recv,
):
    chips = tensors // 2
    s = lax.axis_index("section")
    t = lax.axis_index("tensor")
    c = lax.rem(t, 2)
    m0 = t // 2
    partner = (s, t + 1 - 2 * c)
    rows, feats = emb_ref.shape
    slots = dw_ref.shape[1]
    width = w_ref.shape[2]
    heads = width // HD

    def coef(i, j):
        total = jnp.float32(0.0)
        for k in range(slots):
            total = total + jnp.where(ds_ref[i, k] == j, dw_ref[i, k], jnp.float32(0.0))
        return total

    w_copies = [
        pltpu.make_async_copy(w_hbm.at[j], w_ref.at[j], loc_sem.at[j]) for j in range(3)
    ]
    k_copy = pltpu.make_async_copy(k_hbm, k_ref, loc_sem.at[3])
    v_copy = pltpu.make_async_copy(v_hbm, v_ref, loc_sem.at[4])
    wo_copy = pltpu.make_async_copy(wo_hbm, wo_ref, loc_sem.at[5])
    for cp in w_copies + [k_copy, v_copy, wo_copy]:
        cp.start()

    barrier = pltpu.get_barrier_semaphore()
    for j in range(sections):
        for m in range(chips):

            @pl.when(jnp.logical_or(s != j, m0 != m))
            def _():
                pl.semaphore_signal(
                    barrier, inc=1, device_id=(jnp.int32(j), 2 * m + c), device_id_type=MESH
                )

    pl.semaphore_signal(barrier, inc=1, device_id=partner, device_id_type=MESH)
    pl.semaphore_wait(barrier, sections * chips)

    def own_copy(m):
        return pltpu.make_async_remote_copy(
            src_ref=emb_ref,
            dst_ref=g_ref.at[0, c, m0],
            send_sem=g_send.at[m],
            recv_sem=g_recv.at[0, c, m0],
            device_id=(s, 2 * m + c),
            device_id_type=MESH,
        )

    def partner_copy(src, level, m):
        return pltpu.make_async_remote_copy(
            src_ref=src,
            dst_ref=g_ref.at[level, c, m],
            send_sem=fwd_send.at[level, m],
            recv_sem=g_recv.at[level, c, m],
            device_id=partner,
            device_id_type=MESH,
        )

    def arrive(level, parity, m):
        pltpu.make_async_copy(
            g_ref.at[level, parity, m], g_ref.at[level, parity, m], g_recv.at[level, parity, m]
        ).wait()

    for k in range(1, chips):
        own_copy(lax.rem(m0 + k, chips)).start()
    partner_copy(emb_ref, 0, m0).start()
    g_ref[0, c, m0] = emb_ref[...]
    for k in range(1, chips):
        m = lax.rem(m0 + k, chips)
        arrive(0, c, m)
        partner_copy(g_ref.at[0, c, m], 0, m).start()
    for m in range(chips):
        arrive(0, 1 - c, m)

    cf = coef(s, 0)
    mix_ref[...] = cf * emb_ref[...].astype(F32)
    for tt in range(tensors):
        acc_ref[:, tt * feats : (tt + 1) * feats] = cf * g_ref[0, tt % 2, tt // 2].astype(F32)

    def add_level(level, carry):
        for m in range(chips):
            arrive(level, c, m)
            partner_copy(g_ref.at[level, c, m], level, m).start()
        for m in range(chips):
            arrive(level, 1 - c, m)
        cl = coef(s, level)
        mix_ref[...] = mix_ref[...] + cl * g_ref[level, c, m0].astype(F32)
        for tt in range(tensors):
            cols = slice(tt * feats, (tt + 1) * feats)
            acc_ref[:, cols] = acc_ref[:, cols] + cl * g_ref[level, tt % 2, tt // 2].astype(F32)
        return carry

    lax.fori_loop(1, s + 1, add_level, 0)

    squares = jnp.zeros((rows, HD), F32)
    for tt in range(tensors * feats // HD):
        cols = slice(tt * HD, (tt + 1) * HD)
        avg = acc_ref[:, cols].astype(BF16).astype(F32)
        acc_ref[:, cols] = avg
        squares = squares + avg * avg
        x_ref[:, cols] = (avg * gain_ref[:, cols]).astype(BF16)
    model = tensors * feats
    inv_rms = lax.rsqrt(jnp.sum(squares, axis=1, keepdims=True) / model + 1e-05)

    x = x_ref[...]
    w_copies[0].wait()
    query = (jnp.dot(x, w_ref[0], preferred_element_type=F32) * inv_rms * HD ** (-0.5)).astype(BF16)
    query = query.astype(F32)
    q_ref[...] = query
    w_copies[1].wait()
    key_new = (jnp.dot(x, w_ref[1], preferred_element_type=F32) * inv_rms).astype(BF16).astype(F32)
    w_copies[2].wait()
    value_new = (jnp.dot(x, w_ref[2], preferred_element_type=F32) * inv_rms).astype(BF16).astype(F32)

    cache = k_ref.shape[1]
    head_of_lane = lax.broadcasted_iota(jnp.int32, (SUB, width), 1) // HD
    head_rows = lax.broadcasted_iota(jnp.int32, (SUB, width), 0)
    head_mask = head_of_lane == head_rows
    position = lax.broadcasted_iota(jnp.int32, (SUB, cache), 1)
    group = 8

    k_copy.wait()

    def score_step(step, carry):
        for u in range(group):
            b = step * group + u
            row = order_ref[b]
            qb = jnp.broadcast_to(q_ref[pl.ds(b, 1), :], (SUB, width))
            qb = jnp.where(head_mask, qb, 0.0).astype(BF16)
            sc = lax.dot_general(
                qb, k_ref[row], (((1,), (1,)), ((), ())), preferred_element_type=F32
            )
            s_ref[pl.ds(pl.multiple_of(b * SUB, SUB), SUB), :] = jnp.where(
                position < len_ref[b], sc, -1e30
            )
        return carry

    lax.fori_loop(0, rows // group, score_step, 0)
    p = jnp.exp(s_ref[...])
    d_ref[...] = jnp.broadcast_to(jnp.sum(p, axis=1, keepdims=True), (rows * SUB, HD))
    p_ref[...] = p.astype(BF16).reshape(rows, SUB, cache)

    v_copy.wait()

    def value_step(step, carry):
        for u in range(group):
            b = step * group + u
            row = order_ref[b]
            pv = jnp.dot(p_ref[b], v_ref[row], preferred_element_type=F32)
            for h in range(heads):
                o_ref[h, pl.ds(pl.multiple_of(b * SUB, SUB), SUB), :] = pv[
                    :, h * HD : (h + 1) * HD
                ]
        return carry

    lax.fori_loop(0, rows // group, value_step, 0)

    pieces = []
    for h in range(heads):
        lanes = slice(h * HD, (h + 1) * HD)
        own = jnp.exp(jnp.sum(query[:, lanes] * key_new[:, lanes], axis=1, keepdims=True))
        total = o_ref[h, pl.ds(h, rows, stride=SUB), :]
        total = total + own.astype(BF16).astype(F32) * value_new[:, lanes]
        den = d_ref[pl.ds(h, rows, stride=SUB), :] + own
        pieces.append((total / den).astype(BF16))
    attended = jnp.concatenate(pieces, axis=1)

    def pair_copy(m):
        return pltpu.make_async_remote_copy(
            src_ref=part_ref.at[1 - c, m],
            dst_ref=pair_ref.at[m],
            send_sem=pair_send.at[m],
            recv_sem=pair_recv.at[m],
            device_id=partner,
            device_id_type=MESH,
        )

    def rs_copy(m):
        return pltpu.make_async_remote_copy(
            src_ref=ps_ref.at[m],
            dst_ref=rs_ref.at[m0],
            send_sem=rs_send.at[m],
            recv_sem=rs_recv.at[m0],
            device_id=(s, 2 * m + c),
            device_id_type=MESH,
        )

    wo_copy.wait()
    for m in range(chips):
        both = jnp.dot(
            attended,
            wo_ref[:, 2 * m * feats : 2 * (m + 1) * feats],
            preferred_element_type=F32,
        ).astype(BF16)
        part_ref[0, m] = both[:, :feats]
        part_ref[1, m] = both[:, feats:]
        pair_copy(m).start()
    for m in range(chips):
        pair_copy(m).wait_recv()
        ps_ref[m] = (part_ref[c, m].astype(F32) + pair_ref[m].astype(F32)).astype(BF16)

        @pl.when(m0 != m)
        def _():
            rs_copy(m).start()

    produced = mix_ref[...].astype(BF16).astype(F32) + ps_ref[m0].astype(F32)
    for k in range(1, chips):
        m = lax.rem(m0 + k, chips)
        pltpu.make_async_copy(rs_ref.at[m], rs_ref.at[m], rs_recv.at[m]).wait()
        produced = produced + rs_ref[m].astype(F32)
    outb_ref[...] = produced.astype(BF16)

    def bc_copy(j, m):
        return pltpu.make_async_remote_copy(
            src_ref=outb_ref,
            dst_ref=g_ref.at[s + 1, c, m0],
            send_sem=bc_send.at[j, m],
            recv_sem=g_recv.at[s + 1, c, m0],
            device_id=(j, 2 * m + c),
            device_id_type=MESH,
        )

    def fin_copy(j):
        return pltpu.make_async_remote_copy(
            src_ref=outb_ref,
            dst_ref=fin_ref.at[s],
            send_sem=fin_send.at[j],
            recv_sem=fin_recv.at[s],
            device_id=(j, t),
            device_id_type=MESH,
        )

    def send_later(j, carry):
        for m in range(chips):
            bc_copy(j, m).start()
        return carry

    def send_earlier(j, carry):
        fin_copy(j).start()
        return carry

    lax.fori_loop(s + 1, sections, send_later, 0)
    lax.fori_loop(0, s, send_earlier, 0)

    mix_ref[...] = coef(sections, 0) * emb_ref[...].astype(F32)

    def mix_before(level, carry):
        mix_ref[...] = mix_ref[...] + coef(sections, level) * g_ref[level, c, m0].astype(F32)
        return carry

    lax.fori_loop(1, s + 1, mix_before, 0)
    mix_ref[...] = mix_ref[...] + coef(sections, s + 1) * outb_ref[...].astype(F32)

    def mix_after(j, carry):
        pltpu.make_async_copy(fin_ref.at[j], fin_ref.at[j], fin_recv.at[j]).wait()
        mix_ref[...] = mix_ref[...] + coef(sections, j + 1) * fin_ref[j].astype(F32)
        return carry

    lax.fori_loop(s + 1, sections, mix_after, 0)
    out_rows = out_ref.shape[0]
    for j in range(sections):

        @pl.when(s == j)
        def _():
            out_ref[...] = mix_ref[j * out_rows : (j + 1) * out_rows, :].astype(BF16)

    for k in range(1, chips):
        own_copy(lax.rem(m0 + k, chips)).wait_send()
    for m in range(chips):
        partner_copy(emb_ref, 0, m).wait_send()
        pair_copy(m).wait_send()

        @pl.when(m0 != m)
        def _():
            rs_copy(m).wait_send()

    def drain_forward(level, carry):
        for m in range(chips):
            partner_copy(emb_ref, level, m).wait_send()
        return carry

    def drain_later(j, carry):
        for m in range(chips):
            bc_copy(j, m).wait_send()
        return carry

    def drain_earlier(j, carry):
        fin_copy(j).wait_send()
        return carry

    lax.fori_loop(1, s + 1, drain_forward, 0)
    lax.fori_loop(s + 1, sections, drain_later, 0)
    lax.fori_loop(0, s, drain_earlier, 0)


def per_device(sections, tensors, emb, gain, qkv, wo, ck, cv, dw, ds, order, lengths):
    rows, feats = emb.shape
    model = feats * tensors
    chips = tensors // 2
    w = jnp.transpose(qkv, (0, 2, 1, 3))[0]
    width = w.shape[-1]
    cache = ck.shape[2]
    vmem = pl.BlockSpec(memory_space=pltpu.VMEM)
    smem = pl.BlockSpec(memory_space=pltpu.SMEM)
    hbm = pl.BlockSpec(memory_space=pl.ANY)
    dma = pltpu.SemaphoreType.DMA
    return pl.pallas_call(
        functools.partial(kernel, sections, tensors),
        out_shape=jax.ShapeDtypeStruct((rows // sections, feats), BF16),
        in_specs=[vmem, vmem, hbm, hbm, hbm, hbm, smem, smem, smem, smem],
        out_specs=vmem,
        scratch_shapes=[
            pltpu.VMEM(w.shape, BF16),
            pltpu.VMEM(wo.shape[1:], BF16),
            pltpu.VMEM(ck.shape[1:], BF16),
            pltpu.VMEM(cv.shape[1:], BF16),
            pltpu.VMEM((sections, 2, chips, rows, feats), BF16),
            pltpu.VMEM((sections, rows, feats), BF16),
            pltpu.VMEM((rows, model), F32),
            pltpu.VMEM((rows, model), BF16),
            pltpu.VMEM((rows, width), F32),
            pltpu.VMEM((rows * SUB, cache), F32),
            pltpu.VMEM((rows, SUB, cache), BF16),
            pltpu.VMEM((rows * SUB, HD), F32),
            pltpu.VMEM((width // HD, rows * SUB, HD), F32),
            pltpu.VMEM((2, chips, rows, feats), BF16),
            pltpu.VMEM((chips, rows, feats), BF16),
            pltpu.VMEM((chips, rows, feats), BF16),
            pltpu.VMEM((chips, rows, feats), BF16),
            pltpu.VMEM((rows, feats), BF16),
            pltpu.VMEM((rows, feats), F32),
            dma((6,)),
            dma((sections, 2, chips)),
            dma((chips,)),
            dma((sections, chips)),
            dma((chips,)),
            dma((chips,)),
            dma((chips,)),
            dma((chips,)),
            dma((sections, chips)),
            dma((sections,)),
            dma((sections,)),
        ],
        compiler_params=pltpu.CompilerParams(
            collective_id=0, has_side_effects=True, vmem_limit_bytes=56 * 1024 * 1024
        ),
    )(emb, gain, w, wo[0], ck[0], cv[0], dw, ds, order, lengths)


def solution(mesh):
    placed = (
        P(None, "tensor"),
        P("section", None),
        P("section", None, None, "tensor"),
        P("section", "tensor", None),
        P("section", None, None, "tensor"),
        P("section", None, None, "tensor"),
        P(),
        P(),
        P(),
        P(),
    )
    return jax.shard_map(
        functools.partial(per_device, mesh.shape["section"], mesh.shape["tensor"]),
        mesh=mesh,
        in_specs=placed,
        out_specs=P("section", "tensor"),
        check_vma=False,
    )
```

time: 273 us -> 53.8 us (0.20)
  waiting for transfers between devices: 110 us -> 0 us
  blocking collectives: 61.1 us -> 0 us
  Pallas kernels: 0 us -> 52.3 us
  local copies, waits for them, and re-layouts: 46.8 us -> 1.31 us
  matrix products: 20.8 us -> 0 us
  other arithmetic: 19.3 us -> 0 us
  between operations: 13.4 us -> 0.01 us
    while x4 -> x0, waiting for transfers between devices: 110 us -> none
    pallas_call x0 -> x1, Pallas kernels: none -> 52.3 us  [per_device(): pl.pallas_call(functools.partial(kernel, sections, tensors), out_shape=ja...]
    all_gather x2 -> x0, blocking collectives: 44.6 us -> none  [layer_step(): gathered = lax.all_gather(layer_input, 'tensor', axis=1, tiled=True)]
    dot_general x8 -> x0, matrix products: 20.8 us -> none  [the longest x2 10.8 us: attend(): jnp.dot(normed, qkv_local.reshape(normed.shape[1], -1), preferred_element...]
    while x13 -> x0, local copies, waits for them, and re-layouts: 19.4 us -> none  [the longest x1 12.8 us: per_device(): lax.fori_loop(0, sections, whole_step, (own_coef[0] * start_floats, final...]
    psum x2 -> x0, blocking collectives: 16.6 us -> none  [broadcast(): return lax.psum(jnp.where(mine, value, jnp.zeros_like(value)), axis)]
    reshape x2 -> x0, local copies, waits for them, and re-layouts: 13 us -> none  [attend(): key_rows = key_rows.reshape(row_count, cache_len, heads_here, HD)]
    gather x2 -> x0, local copies, waits for them, and re-layouts: 10.1 us -> none  [the longest x1 5.07 us: layer_step(): key_rows = jnp.take(cache_keys[0], token_order, axis=0)]
  transfers between devices with their start and end apart: 2 -> 0, of which waited for: 2 -> 0; matrix products, arithmetic and copies ran while one was open for 1% -> 0% of each run, Pallas kernels for 0% -> 0%
where the time goes in v1:
time: 53.8 us; the launch traced here: 53.6 us
  Pallas kernels  52.3 us (97%)
  local copies, waits for them, and re-layouts  1.31 us (2%)
    pallas_call x1, Pallas kernels, per_device(): pl.pallas_call(functools.partial(kernel, sections, tensors), out_shape=ja...  52.3 us
    unnamed x1, local copies, waits for them, and re-layouts  1.31 us

profile of v1, /device:TPU:0, one launch (start us, length us, event | category | flops | bytes accessed | tf_op | source)
XLA Modules:
  0.0 53.6 jit_solution(14486644589088281487)
XLA Ops:
  0.0 52.3 %shard_map.100 = bf16[16,384]{1,0:T(8,128)(2,1)} custom-call(bf16[32,384]{1,0:T(8,128)(2,1)} %emb_ref.1, f32[1,6144]{1,0:T(1,128)} %gain_ref.1, bf16[3,6144,256]{2,1,0:T(8,128)(2,1)} %bitcast.6, bf16[256,6144]{1,0:T(8,128)(2,1)} %bitcast.9, bf16[32,256,256]{2,1,0:T(8,128)(2,1)} %bitcast.7, bf16[32,256,256]{2,1,0:T(8,128)(2,1)} %bitcast.8, f32[3,4]{1,0:T(4,128)} %dw_ref.1, ...), custom_call_target="tpu_custom_call" | custom-call | tf_op jit(solution)/shard_map/pallas_call | solution.py:369
  52.3 1.3 %copy.12 = bf16[16,384]{1,0:T(8,128)(2,1)} copy(bf16[16,384]{1,0:T(8,128)(2,1)} %shard_map.100) | data formatting | bytes 24576

commit v2 on v1

v2 whole, which is shorter than its diff:
```python
import functools

import jax
import jax.numpy as jnp
from jax import lax
from jax.experimental import pallas as pl
from jax.experimental.pallas import tpu as pltpu
from jax.sharding import PartitionSpec as P

HD = 128
SUB = 8
MESH = pl.DeviceIdType.MESH
F32 = jnp.float32
BF16 = jnp.bfloat16


def kernel(
    sections,
    tensors,
    emb_ref,
    gain_ref,
    w_hbm,
    wo_hbm,
    k_hbm,
    v_hbm,
    dw_ref,
    ds_ref,
    order_ref,
    len_ref,
    out_ref,
    w_ref,
    wo_ref,
    k_ref,
    v_ref,
    g_ref,
    fin_ref,
    acc_ref,
    x_ref,
    q_ref,
    s_ref,
    p_ref,
    d_ref,
    o_ref,
    part_ref,
    pair_ref,
    ps_ref,
    rs_ref,
    fps_ref,
    frs_ref,
    outb_ref,
    mix_ref,
    avl_ref,
    loc_sem,
    g_recv,
    g_send,
    fwd_send,
    pair_send,
    pair_recv,
    rs_send,
    rs_recv,
    frs_send,
    frs_recv,
    bc_send,
    fin_send,
    fin_recv,
    ready_sem,
):
    chips = tensors // 2
    last = sections - 1
    s = lax.axis_index("section")
    t = lax.axis_index("tensor")
    c = lax.rem(t, 2)
    m0 = t // 2
    partner = (s, t + 1 - 2 * c)
    rows, feats = emb_ref.shape
    slots = dw_ref.shape[1]
    width = w_ref.shape[3]
    heads = width // HD

    def coef(i, j):
        total = jnp.float32(0.0)
        for k in range(slots):
            total = total + jnp.where(ds_ref[i, k] == j, dw_ref[i, k], jnp.float32(0.0))
        return total

    def remote(src, dst, send, recv, device):
        return pltpu.make_async_remote_copy(
            src_ref=src,
            dst_ref=dst,
            send_sem=send,
            recv_sem=recv,
            device_id=device,
            device_id_type=MESH,
        )

    def landed(ref, sem):
        pltpu.make_async_copy(ref, ref, sem).wait()

    barrier = pltpu.get_barrier_semaphore()
    pl.semaphore_signal(barrier, inc=1, device_id=partner, device_id_type=MESH)
    for k in range(1, chips):
        m = lax.rem(m0 + k, chips)
        pl.semaphore_signal(barrier, inc=1, device_id=(s, 2 * m + c), device_id_type=MESH)
    for k in range(1, sections):
        j = lax.rem(s + k, sections)
        pl.semaphore_signal(barrier, inc=1, device_id=(j, t), device_id_type=MESH)

    w_copies = [
        pltpu.make_async_copy(w_hbm.at[j], w_ref.at[j], loc_sem.at[j]) for j in range(3)
    ]
    k_copy = pltpu.make_async_copy(k_hbm, k_ref, loc_sem.at[3])
    v_copy = pltpu.make_async_copy(v_hbm, v_ref, loc_sem.at[4])
    wo_copy = pltpu.make_async_copy(wo_hbm, wo_ref, loc_sem.at[5])
    for cp in w_copies + [k_copy, v_copy, wo_copy]:
        cp.start()
    acc_ref[...] = jnp.zeros_like(acc_ref)

    pl.semaphore_wait(barrier, chips + sections - 1)
    for k in range(1, sections):
        j = lax.rem(s + k, sections)
        pl.semaphore_signal(ready_sem, inc=1, device_id=(j, t), device_id_type=MESH)

    def spread(src, level, group, m):
        return remote(
            src,
            g_ref.at[level, c, m0],
            g_send.at[group, m],
            g_recv.at[level, c, m0],
            (s, 2 * m + c),
        )

    def forward(src, level, m):
        return remote(
            src, g_ref.at[level, c, m], fwd_send.at[level, m], g_recv.at[level, c, m], partner
        )

    def arrive(level, parity, m):
        landed(g_ref.at[level, parity, m], g_recv.at[level, parity, m])

    def spread_start(src, level, group):
        for k in range(1, chips):
            spread(src, level, group, lax.rem(m0 + k, chips)).start()
        forward(src, level, m0).start()
        g_ref[level, c, m0] = src[...]

    def to_later(j, m):
        return remote(
            outb_ref,
            g_ref.at[s, c, m0],
            bc_send.at[j, m],
            g_recv.at[s, c, m0],
            (j, 2 * m + c),
        )

    def to_earlier(j):
        return remote(outb_ref, fin_ref.at[s], fin_send.at[j], fin_recv.at[s], (j, t))

    @pl.when(s == 0)
    def _():
        outb_ref[...] = emb_ref[...]

    @pl.when(s > 0)
    def _():
        spread_start(emb_ref, 0, 0)

        def add_level(level, carry):
            for k in range(chips):
                m = lax.rem(m0 + k, chips)
                if k == 0:

                    @pl.when(level > 0)
                    def _():
                        arrive(level, c, m)
                        forward(g_ref.at[level, c, m], level, m).start()
                else:
                    arrive(level, c, m)
                    forward(g_ref.at[level, c, m], level, m).start()
            for m in range(chips):
                arrive(level, 1 - c, m)
            cl = coef(s, level)
            for m in range(chips):
                for par in range(2):
                    acc_ref[par, m] = acc_ref[par, m] + cl * g_ref[level, par, m].astype(F32)
            return carry

        lax.fori_loop(0, s, add_level, 0)

        mix_ref[...] = jnp.zeros_like(mix_ref)

        def add_below(level, carry):
            mix_ref[...] = mix_ref[...] + coef(s - 1, level) * g_ref[level, c, m0].astype(F32)
            return carry

        lax.fori_loop(0, s, add_below, 0)
        produced = mix_ref[...].astype(BF16).astype(F32)
        for k in range(chips):
            m = lax.rem(m0 + k, chips)
            landed(rs_ref.at[m], rs_recv.at[m])
            produced = produced + rs_ref[m].astype(F32)
        outb_ref[...] = produced.astype(BF16)

    spread_start(outb_ref, s, 1)
    pl.semaphore_wait(ready_sem, sections - 1)

    @pl.when(s > 0)
    def _():
        def send_later(j, carry):
            for m in range(chips):
                to_later(j, m).start()
            return carry

        def send_earlier(j, carry):
            to_earlier(j).start()
            return carry

        lax.fori_loop(s + 1, sections, send_later, 0)
        lax.fori_loop(0, s, send_earlier, 0)

    top = coef(s, s)
    squares = jnp.zeros((rows, 1), F32)
    proj = [jnp.zeros((rows, width), F32) for _ in range(3)]
    lag = 2
    for k in range(chips + lag):
        if 0 < k < chips:
            m = lax.rem(m0 + k, chips)
            arrive(s, c, m)
            forward(g_ref.at[s, c, m], s, m).start()
        k = k - lag
        if k < 0:
            continue
        m = lax.rem(m0 + k, chips)
        arrive(s, 1 - c, m)
        gains = gain_ref[:, pl.ds(pl.multiple_of(m * 2 * feats, HD), 2 * feats)]
        for par in range(2):
            cols = slice(par * feats, (par + 1) * feats)
            avg = acc_ref[par, m] + top * g_ref[s, par, m].astype(F32)
            avg = avg.astype(BF16).astype(F32)
            squares = squares + jnp.sum(avg * avg, axis=1, keepdims=True)
            x_ref[k, :, cols] = (avg * gains[:, cols]).astype(BF16)
        if k == 0:
            for cp in w_copies:
                cp.wait()
        x = x_ref[k]
        for j in range(3):
            proj[j] = proj[j] + jnp.dot(x, w_ref[j, m], preferred_element_type=F32)
    inv_rms = lax.rsqrt(squares / (tensors * feats) + 1e-05)
    query = (proj[0] * inv_rms * HD ** (-0.5)).astype(BF16).astype(F32)
    q_ref[...] = query
    key_new = (proj[1] * inv_rms).astype(BF16).astype(F32)
    value_new = (proj[2] * inv_rms).astype(BF16).astype(F32)

    cache = k_ref.shape[1]
    head_of_lane = lax.broadcasted_iota(jnp.int32, (SUB, width), 1) // HD
    head_rows = lax.broadcasted_iota(jnp.int32, (SUB, width), 0)
    head_mask = head_of_lane == head_rows
    position = lax.broadcasted_iota(jnp.int32, (SUB, cache), 1)
    group = 8

    k_copy.wait()

    def score_step(step, carry):
        for u in range(group):
            b = step * group + u
            row = order_ref[b]
            qb = jnp.broadcast_to(q_ref[pl.ds(b, 1), :], (SUB, width))
            qb = jnp.where(head_mask, qb, 0.0).astype(BF16)
            sc = lax.dot_general(
                qb, k_ref[row], (((1,), (1,)), ((), ())), preferred_element_type=F32
            )
            s_ref[pl.ds(pl.multiple_of(b * SUB, SUB), SUB), :] = jnp.where(
                position < len_ref[b], sc, -1e30
            )
        return carry

    lax.fori_loop(0, rows // group, score_step, 0)
    p = jnp.exp(s_ref[...])
    d_ref[...] = jnp.broadcast_to(jnp.sum(p, axis=1, keepdims=True), (rows * SUB, HD))
    p_ref[...] = p.astype(BF16).reshape(rows, SUB, cache)

    v_copy.wait()

    def value_step(step, carry):
        for u in range(group):
            b = step * group + u
            row = order_ref[b]
            pv = jnp.dot(p_ref[b], v_ref[row], preferred_element_type=F32)
            for h in range(heads):
                o_ref[h, pl.ds(pl.multiple_of(b * SUB, SUB), SUB), :] = pv[
                    :, h * HD : (h + 1) * HD
                ]
        return carry

    lax.fori_loop(0, rows // group, value_step, 0)

    pieces = []
    for h in range(heads):
        lanes = slice(h * HD, (h + 1) * HD)
        own = jnp.exp(jnp.sum(query[:, lanes] * key_new[:, lanes], axis=1, keepdims=True))
        total = o_ref[h, pl.ds(h, rows, stride=SUB), :]
        total = total + own.astype(BF16).astype(F32) * value_new[:, lanes]
        den = d_ref[pl.ds(h, rows, stride=SUB), :] + own
        pieces.append((total / den).astype(BF16))
    attended = jnp.concatenate(pieces, axis=1)

    def pair_copy(m):
        return remote(
            part_ref.at[1 - c, m], pair_ref.at[m], pair_send.at[m], pair_recv.at[m], partner
        )

    def rs_copy(m):
        return remote(
            ps_ref.at[m], rs_ref.at[m0], rs_send.at[m], rs_recv.at[m0], (s + 1, 2 * m + c)
        )

    def frs_copy(j, m):
        return remote(
            fps_ref.at[j, m],
            frs_ref.at[m0],
            frs_send.at[j, m],
            frs_recv.at[m0],
            (jnp.int32(j), 2 * m + c),
        )

    wo_copy.wait()
    for m in range(chips):
        both = jnp.dot(
            attended,
            wo_ref[:, 2 * m * feats : 2 * (m + 1) * feats],
            preferred_element_type=F32,
        ).astype(BF16)
        part_ref[0, m] = both[:, :feats]
        part_ref[1, m] = both[:, feats:]
        pair_copy(m).start()

    out_rows = out_ref.shape[0]

    def pair_sum(m):
        pair_copy(m).wait_recv()
        return part_ref[c, m].astype(F32) + pair_ref[m].astype(F32)

    @pl.when(s < last)
    def _():
        for m in range(chips):
            ps_ref[m] = pair_sum(m).astype(BF16)
            rs_copy(m).start()

    @pl.when(s == last)
    def _():
        for m in range(chips):
            total = pair_sum(m)
            for j in range(sections):
                fps_ref[j, m] = total[j * out_rows : (j + 1) * out_rows].astype(BF16)
                if j < last:
                    frs_copy(j, m).start()
                else:

                    @pl.when(m0 != m)
                    def _():
                        frs_copy(j, m).start()

    base = emb_ref[...].astype(F32)
    mix_ref[...] = coef(sections, 0) * base
    avl_ref[...] = coef(last, 0) * base

    def mix_in(level, value):
        value = value.astype(F32)
        mix_ref[...] = mix_ref[...] + coef(sections, level) * value
        avl_ref[...] = avl_ref[...] + coef(last, level) * value

    def mix_before(level, carry):
        mix_in(level, g_ref[level, c, m0])
        return carry

    def mix_after(level, carry):
        landed(fin_ref.at[level], fin_recv.at[level])
        mix_in(level, fin_ref[level])
        return carry

    lax.fori_loop(1, s + 1, mix_before, 0)
    lax.fori_loop(s + 1, sections, mix_after, 0)

    @pl.when(s == last)
    def _():
        frs_ref[m0] = fps_ref[last, m0]

    top_out = coef(sections, sections)
    for k in range(chips):
        m = lax.rem(m0 + k, chips)
        if k == 0:

            @pl.when(s < last)
            def _():
                landed(frs_ref.at[m], frs_recv.at[m])

            summed = frs_ref[m].astype(F32)
        else:
            landed(frs_ref.at[m], frs_recv.at[m])
            summed = summed + frs_ref[m].astype(F32)
    for j in range(sections):

        @pl.when(s == j)
        def _():
            mine = slice(j * out_rows, (j + 1) * out_rows)
            final = (avl_ref[mine, :].astype(BF16).astype(F32) + summed).astype(BF16)
            out_ref[...] = (mix_ref[mine, :] + top_out * final.astype(F32)).astype(BF16)

    for k in range(1, chips):
        spread(outb_ref, s, 1, lax.rem(m0 + k, chips)).wait_send()
    for m in range(chips):
        pair_copy(m).wait_send()

    @pl.when(s > 0)
    def _():
        for k in range(1, chips):
            spread(emb_ref, 0, 0, lax.rem(m0 + k, chips)).wait_send()

    @pl.when(s < last)
    def _():
        for m in range(chips):
            rs_copy(m).wait_send()

    @pl.when(s == last)
    def _():
        for m in range(chips):
            for j in range(sections):
                if j < last:
                    frs_copy(j, m).wait_send()
                else:

                    @pl.when(m0 != m)
                    def _():
                        frs_copy(j, m).wait_send()

    def drain_forward(level, carry):
        for m in range(chips):
            forward(emb_ref, level, m).wait_send()
        return carry

    def drain_later(j, carry):
        for m in range(chips):
            to_later(j, m).wait_send()
        return carry

    def drain_earlier(j, carry):
        to_earlier(j).wait_send()
        return carry

    lax.fori_loop(0, s + 1, drain_forward, 0)

    @pl.when(s > 0)
    def _():
        lax.fori_loop(s + 1, sections, drain_later, 0)
        lax.fori_loop(0, s, drain_earlier, 0)


def per_device(sections, tensors, emb, gain, qkv, wo, ck, cv, dw, ds, order, lengths):
    rows, feats = emb.shape
    chips = tensors // 2
    w = jnp.transpose(qkv, (0, 2, 1, 3))[0].reshape(3, chips, 2 * feats, -1)
    width = w.shape[-1]
    cache = ck.shape[2]
    vmem = pl.BlockSpec(memory_space=pltpu.VMEM)
    smem = pl.BlockSpec(memory_space=pltpu.SMEM)
    hbm = pl.BlockSpec(memory_space=pl.ANY)
    dma = pltpu.SemaphoreType.DMA
    return pl.pallas_call(
        functools.partial(kernel, sections, tensors),
        out_shape=jax.ShapeDtypeStruct((rows // sections, feats), BF16),
        in_specs=[vmem, vmem, hbm, hbm, hbm, hbm, smem, smem, smem, smem],
        out_specs=vmem,
        scratch_shapes=[
            pltpu.VMEM(w.shape, BF16),
            pltpu.VMEM(wo.shape[1:], BF16),
            pltpu.VMEM(ck.shape[1:], BF16),
            pltpu.VMEM(cv.shape[1:], BF16),
            pltpu.VMEM((sections, 2, chips, rows, feats), BF16),
            pltpu.VMEM((sections, rows, feats), BF16),
            pltpu.VMEM((2, chips, rows, feats), F32),
            pltpu.VMEM((chips, rows, 2 * feats), BF16),
            pltpu.VMEM((rows, width), F32),
            pltpu.VMEM((rows * SUB, cache), F32),
            pltpu.VMEM((rows, SUB, cache), BF16),
            pltpu.VMEM((rows * SUB, HD), F32),
            pltpu.VMEM((width // HD, rows * SUB, HD), F32),
            pltpu.VMEM((2, chips, rows, feats), BF16),
            pltpu.VMEM((chips, rows, feats), BF16),
            pltpu.VMEM((chips, rows, feats), BF16),
            pltpu.VMEM((chips, rows, feats), BF16),
            pltpu.VMEM((sections, chips, rows // sections, feats), BF16),
            pltpu.VMEM((chips, rows // sections, feats), BF16),
            pltpu.VMEM((rows, feats), BF16),
            pltpu.VMEM((rows, feats), F32),
            pltpu.VMEM((rows, feats), F32),
            dma((6,)),
            dma((sections, 2, chips)),
            dma((2, chips)),
            dma((sections, chips)),
            dma((chips,)),
            dma((chips,)),
            dma((chips,)),
            dma((chips,)),
            dma((sections, chips)),
            dma((chips,)),
            dma((sections, chips)),
            dma((sections,)),
            dma((sections,)),
            pltpu.SemaphoreType.REGULAR,
        ],
        compiler_params=pltpu.CompilerParams(
            collective_id=0, has_side_effects=True, vmem_limit_bytes=56 * 1024 * 1024
        ),
    )(emb, gain, w, wo[0], ck[0], cv[0], dw, ds, order, lengths)


def solution(mesh):
    placed = (
        P(None, "tensor"),
        P("section", None),
        P("section", None, None, "tensor"),
        P("section", "tensor", None),
        P("section", None, None, "tensor"),
        P("section", None, None, "tensor"),
        P(),
        P(),
        P(),
        P(),
    )
    return jax.shard_map(
        functools.partial(per_device, mesh.shape["section"], mesh.shape["tensor"]),
        mesh=mesh,
        in_specs=placed,
        out_specs=P("section", "tensor"),
        check_vma=False,
    )
```

time: 53.8 us -> 50 us (0.929)
  Pallas kernels: 52.3 us -> 48.4 us
    pallas_call x1, Pallas kernels: 52.3 us -> 48.4 us  [per_device(): pl.pallas_call(functools.partial(kernel, sections, tensors), out_shape=ja...]
where the time goes in v2:
time: 50 us; the launch traced here: 49.7 us
  Pallas kernels  48.4 us (97%)
  local copies, waits for them, and re-layouts  1.31 us (3%)
    pallas_call x1, Pallas kernels, per_device(): pl.pallas_call(functools.partial(kernel, sections, tensors), out_shape=ja...  48.4 us
    unnamed x1, local copies, waits for them, and re-layouts  1.31 us

profile of v2, /device:TPU:0, one launch (start us, length us, event | category | flops | bytes accessed | tf_op | source)
XLA Modules:
  0.0 49.7 jit_solution(14091076670112198995)
XLA Ops:
  0.0 48.4 %shard_map.100 = bf16[16,384]{1,0:T(8,128)(2,1)} custom-call(bf16[32,384]{1,0:T(8,128)(2,1)} %emb_ref.1, f32[1,6144]{1,0:T(1,128)} %gain_ref.1, bf16[3,8,768,256]{3,2,1,0:T(8,128)(2,1)} %bitcast.6, bf16[256,6144]{1,0:T(8,128)(2,1)} %bitcast.9, bf16[32,256,256]{2,1,0:T(8,128)(2,1)} %bitcast.7, bf16[32,256,256]{2,1,0:T(8,128)(2,1)} %bitcast.8, f32[3,4]{1,0:T(4,128)} %dw_ref.1, ...), custom_call_target="tpu_custom_call" | custom-call | tf_op jit(solution)/shard_map/pallas_call | solution.py:466
  48.4 1.3 %copy.12 = bf16[16,384]{1,0:T(8,128)(2,1)} copy(bf16[16,384]{1,0:T(8,128)(2,1)} %shard_map.100) | data formatting | bytes 24576

commit v3 on v2

--- a/solution.py
+++ b/solution.py
@@ -219,7 +219,7 @@
     top = coef(s, s)
     squares = jnp.zeros((rows, 1), F32)
     proj = [jnp.zeros((rows, width), F32) for _ in range(3)]
-    lag = 2
+    lag = chips
     for k in range(chips + lag):
         if 0 < k < chips:
             m = lax.rem(m0 + k, chips)
@@ -254,7 +254,7 @@
     head_rows = lax.broadcasted_iota(jnp.int32, (SUB, width), 0)
     head_mask = head_of_lane == head_rows
     position = lax.broadcasted_iota(jnp.int32, (SUB, cache), 1)
-    group = 8
+    group = rows
 
     k_copy.wait()
 
@@ -330,7 +330,9 @@
         ).astype(BF16)
         part_ref[0, m] = both[:, :feats]
         part_ref[1, m] = both[:, feats:]
-        pair_copy(m).start()
+        if m % 4 == 3:
+            for i in range(m - 3, m + 1):
+                pair_copy(i).start()
 
     out_rows = out_ref.shape[0]
 

time: 50 us -> 45.8 us (0.916)
  Pallas kernels: 48.4 us -> 44.3 us
    pallas_call x1, Pallas kernels: 48.4 us -> 44.3 us  [per_device(): pl.pallas_call(functools.partial(kernel, sections, tensors), out_shape=ja...]
where the time goes in v3:
time: 45.8 us; the launch traced here: 45.6 us
  Pallas kernels  44.3 us (97%)
  local copies, waits for them, and re-layouts  1.31 us (3%)
    pallas_call x1, Pallas kernels, per_device(): pl.pallas_call(functools.partial(kernel, sections, tensors), out_shape=ja...  44.3 us
    unnamed x1, local copies, waits for them, and re-layouts  1.31 us

profile of v3, /device:TPU:0, one launch (start us, length us, event | category | flops | bytes accessed | tf_op | source)
XLA Modules:
  0.0 45.6 jit_solution(2830873578752291868)
XLA Ops:
  0.0 44.3 %shard_map.100 = bf16[16,384]{1,0:T(8,128)(2,1)} custom-call(bf16[32,384]{1,0:T(8,128)(2,1)} %emb_ref.1, f32[1,6144]{1,0:T(1,128)} %gain_ref.1, bf16[3,8,768,256]{3,2,1,0:T(8,128)(2,1)} %bitcast.6, bf16[256,6144]{1,0:T(8,128)(2,1)} %bitcast.9, bf16[32,256,256]{2,1,0:T(8,128)(2,1)} %bitcast.7, bf16[32,256,256]{2,1,0:T(8,128)(2,1)} %bitcast.8, f32[3,4]{1,0:T(4,128)} %dw_ref.1, ...), custom_call_target="tpu_custom_call" | custom-call | tf_op jit(solution)/shard_map/pallas_call | solution.py:468
  44.3 1.3 %copy.12 = bf16[16,384]{1,0:T(8,128)(2,1)} copy(bf16[16,384]{1,0:T(8,128)(2,1)} %shard_map.100) | data formatting | bytes 24576
